TPU v7x, 32 devices: a whole 2x2x4 slice. The times are simulated.
32 devices in a mesh: grp: 4 (over z), row: 4 (over y, core), col: 2 (over x).
Axes of the slice: x: 2, y: 2, z: 4, core: 2. Of those that a mesh axis runs over, the one named last changes fastest.
Arguments:
- tokens: bfloat16 [2048, 4608], P(('grp', 'row', 'col')), parts along dimension 0, may hold values from -6 to 6
- ln_gain: float32 [4608], replicated, may hold values from 0.1 to 1.9
- w_in: bfloat16 [4608, 12288], P('row', 'col'), may hold values from -0.09375 to 0.09375
- b_in: float32 [12288], P('col'), may hold values from -3 to 3
- w_out: bfloat16 [12288, 4608], P('col', 'row'), may hold values from -0.0546875 to 0.0546875
- b_out: float32 [4608], P('row'), may hold values from -3 to 3
Outputs:
- result: bfloat16 [2048, 4608], P(('grp', 'row', 'col')), parts along dimension 0
There are 4 independent parts, one for each index of `grp`. A program takes and returns all parts, laid end to end along the dimension named above; an argument that names none is the same for every part. Nothing has to cross between parts.
All inputs are finite; a program needn't handle non-finite values.
Results may differ from a plain program's by a relative error of at most 0.0095.
Values may be sent and summed in bfloat16 or wider, within the bound.
A program may use at most 128 MiB of HBM per device.

v0:
```python
import jax
import jax.numpy as jnp
from jax import lax
from jax.sharding import PartitionSpec as P


def local(tokens, ln_gain, w_in, b_in, w_out, b_out):
    values = tokens.astype(jnp.float32)
    row_mean = jnp.mean(values, axis=1, keepdims=True)
    centered = values - row_mean
    row_var = jnp.mean(centered * centered, axis=1, keepdims=True)
    normed = (centered * lax.rsqrt(row_var + 1e-06) * ln_gain).astype(jnp.bfloat16)
    own_cols = lax.all_to_all(normed, "row", split_axis=1, concat_axis=0, tiled=True)
    partial_pre = jnp.dot(
        lax.all_gather(own_cols, "col", axis=0, tiled=True),
        w_in,
        preferred_element_type=jnp.float32,
    )
    preact = lax.psum_scatter(partial_pre, "row", scatter_dimension=0, tiled=True) + b_in
    hidden = jax.nn.gelu(preact, approximate=False).astype(jnp.bfloat16)
    down_part = jnp.dot(
        lax.all_gather(hidden, "row", axis=0, tiled=True), w_out, preferred_element_type=jnp.float32
    )
    summed = lax.psum_scatter(
        down_part.astype(jnp.bfloat16), "col", scatter_dimension=0, tiled=True
    ).astype(jnp.float32)
    branch_out = (summed + b_out).astype(jnp.bfloat16)
    regrouped = lax.all_to_all(branch_out, "row", split_axis=0, concat_axis=1, tiled=True)
    return (values + regrouped.astype(jnp.float32)).astype(jnp.bfloat16)


def solution(mesh):
    in_specs = (
        P(("grp", "row", "col"), None),
        P(),
        P("row", "col"),
        P("col"),
        P("col", "row"),
        P("row"),
    )
    out_specs = P(("grp", "row", "col"), None)
    return jax.shard_map(local, mesh=mesh, in_specs=in_specs, out_specs=out_specs, check_vma=False)
```

profile of v0, /device:TPU:0, one launch (start us, length us, event | category | flops | bytes accessed | tf_op | source)
XLA Modules:
  0.0 273.9 jit_solution(3473818325535875934)
XLA Ops:
  6.5 0.0 all-gather.3.cloned.1.call-start
  6.5 1.2 convert_reduce_fusion
  7.8 1.4 fusion.12
  9.2 1.3 fusion.14
  10.6 13.7 %all_to_all.32 = bf16[64,4,1152]{2,0,1:T(8,128)(2,1)} all-to-all(bf16[64,4,1152]{2,0,1:T(8,128)(2,1)S(1)} %bitcast.19), channel_id=1, replica_groups=mesh['grp'=4,'row'=4,'col'=2] {'row'}, dimensions={1} | all-to-all | bytes 1179648 | tf_op jit(solution)/shard_map/all_to_all | solution.py:13
  24.3 0.0 all-gather.3.cloned.1.call-update
  24.3 0.0 reduce-scatter.3.cloned.1.call-start
  24.3 23.6 %all-gather.3.cloned.1.call-done = bf16[512,1152]{1,0:T(8,128)(2,1)} async-done(((bf16[256,1152]{1,0:T(8,128)(2,1)}), bf16[512,1152]{1,0:T(8,128)(2,1)}) %all-gather.3.cloned.1.call-update) | async-done | bytes 1179664 | tf_op jit(solution)/shard_map/all_gather | solution.py:15
  47.9 14.4 %fusion.16 = f32[512,6144]{1,0:T(8,128)} fusion(bf16[512,1152]{1,0:T(8,128)(2,1)} %all-gather.3.cloned.1.call-done, bf16[1152,6144]{1,0:T(8,128)(2,1)} %param.8), kind=kOutput, calls=%fused_computation.34 | convolution fusion | flops 7247757312 | bytes 27918336 | tf_op jit(solution)/shard_map/dot_general | solution.py:14
  62.3 0.0 copy-start.1
  62.3 0.0 reduce-scatter.3.cloned.1.call-update
  62.3 0.0 all-gather.5.cloned.1.call-start
  62.4 99.7 %reduce-scatter.3.cloned.1.call-done = f32[128,6144]{1,0:T(8,128)} async-done(((f32[512,6144]{1,0:T(8,128)}), f32[128,6144]{1,0:T(8,128)}) %reduce-scatter.3.cloned.1.call-update) | async-done | bytes 3145744 | tf_op jit(solution)/shard_map/reduce_scatter | solution.py:19
  162.1 0.0 copy-done.1
  162.1 8.8 %fusion.2 = bf16[128,6144]{1,0:T(8,128)(2,1)} fusion(f32[128,6144]{1,0:T(8,128)} %reduce-scatter.3.cloned.1.call-done, f32[6144]{0:T(1024)S(1)} %copy-done.1), kind=kLoop, calls=%fused_computation.3 | loop fusion | flops 51904512 | bytes 4743168 | tf_op jit(solution)/shard_map/convert_element_type | solution.py:20
  170.9 0.0 all-gather.5.cloned.1.call-update
  170.9 0.0 copy-start.2
  170.9 0.0 reduce-scatter.5.cloned.1.call-start
  171.0 46.4 %all-gather.5.cloned.1.call-done = bf16[512,6144]{1,0:T(8,128)(2,1)} async-done(((bf16[128,6144]{1,0:T(8,128)(2,1)}), bf16[512,6144]{1,0:T(8,128)(2,1)}) %all-gather.5.cloned.1.call-update) | async-done | bytes 6291472 | tf_op jit(solution)/shard_map/all_gather | solution.py:22
  217.4 13.6 %convolution_convert_fusion = bf16[512,1152]{1,0:T(8,128)(2,1)} fusion(bf16[512,6144]{1,0:T(8,128)(2,1)} %all-gather.5.cloned.1.call-done, bf16[6144,1152]{1,0:T(8,128)(2,1)} %param.10), kind=kOutput, calls=%fused_computation.19 | convolution fusion | flops 7248347136 | bytes 21626880 | tf_op jit(solution)/shard_map/dot_general | solution.py:21
  231.0 0.0 reduce-scatter.5.cloned.1.call-update
  231.0 0.0 copy-start
  231.0 22.0 %reduce-scatter.5.cloned.1.call-done = bf16[256,1152]{1,0:T(8,128)(2,1)} async-done(((bf16[512,1152]{1,0:T(8,128)(2,1)}), bf16[256,1152]{1,0:T(8,128)(2,1)}) %reduce-scatter.5.cloned.1.call-update) | async-done | bytes 589840 | tf_op jit(solution)/shard_map/reduce_scatter | solution.py:24
  253.0 0.0 copy-done.2
  253.0 1.2 add_convert_fusion
  254.1 12.1 %all_to_all.33 = bf16[4,64,1152]{2,1,0:T(8,128)(2,1)S(1)} all-to-all(bf16[4,64,1152]{2,1,0:T(8,128)(2,1)S(1)} %bitcast.20), channel_id=1, replica_groups=mesh['grp'=4,'row'=4,'col'=2] {'row'}, dimensions={0} | all-to-all | bytes 1179648 | tf_op jit(solution)/shard_map/all_to_all | solution.py:28
  266.2 0.1 convert_bitcast_fusion
  266.3 0.1 copy.14
  266.4 0.0 copy-done
  266.4 0.9 fusion.15
  (3 shorter events, 0.1 us)
Async XLA Ops:
  6.5 41.3 %all-gather.3.cloned.1.call-start = ((), (), s32[]{:S(2)}) async-start(), calls=%async_computation.4 | async-start | bytes 1769472 | tf_op jit(solution)/shard_map/all_gather | solution.py:15
  24.3 137.8 %reduce-scatter.3.cloned.1.call-start = ((), (), s32[]{:S(2)}) async-start(), calls=%async_computation.5 | async-start | bytes 15728640 | tf_op jit(solution)/shard_map/reduce_scatter | solution.py:19
  62.3 99.8 %copy-start.1 = (f32[6144]{0:T(1024)S(1)}, f32[6144]{0:T(1024)}, u32[]{:S(2)}) copy-start(f32[6144]{0:T(1024)} %param.9) | copy-start | bytes 73732
  62.3 155.1 %all-gather.5.cloned.1.call-start = ((), (), s32[]{:S(2)}) async-start(), calls=%async_computation.6 | async-start | bytes 7864320 | tf_op jit(solution)/shard_map/all_gather | solution.py:22
  170.9 82.1 %copy-start.2 = (f32[1152]{0:T(1024)S(1)}, f32[1152]{0:T(1024)}, u32[]{:S(2)}) copy-start(f32[1152]{0:T(1024)} %param.11) | copy-start | bytes 13828
  170.9 82.0 %reduce-scatter.5.cloned.1.call-start = ((), (), s32[]{:S(2)}) async-start(), calls=%async_computation.7 | async-start | bytes 1769472 | tf_op jit(solution)/shard_map/reduce_scatter | solution.py:24
  231.0 35.4 %copy-start = (bf16[64,4608]{1,0:T(8,128)(2,1)S(1)}, bf16[64,4608]{1,0:T(8,128)(2,1)}, u32[]{:S(2)}) copy-start(bf16[64,4608]{1,0:T(8,128)(2,1)} %param.6) | copy-start | bytes 1769476
Sparse Core Ops, SparseCore 0:
  24.4 23.4 all-gather.2
  62.5 99.6 reduce-scatter.2
  171.0 46.3 all-gather.4
  231.1 21.8 reduce-scatter.4
where the time goes:
time: 274 us
  waiting for transfers between devices  192 us (70%)
  matrix products  28 us (10%)
  blocking collectives  25.8 us (9%)
  other arithmetic  14.9 us (5%)
  between operations  13.2 us (5%)
    reduce_scatter x1, waiting for transfers between devices, local(): lax.psum_scatter(partial_pre, 'row', scatter_dimension=0, tiled=True) + b_in  99.7 us
    all_gather x1, waiting for transfers between devices, local(): lax.all_gather(hidden, 'row', axis=0, tiled=True)  46.4 us
    all_gather x1, waiting for transfers between devices, local(): lax.all_gather(own_cols, 'col', axis=0, tiled=True)  23.6 us
    reduce_scatter x1, waiting for transfers between devices, local(): lax.psum_scatter(down_part.astype(jnp.bfloat16), 'col', scatter_dimension...  22 us
    dot_general x1, matrix products, local(): jnp.dot(lax.all_gather(own_cols, 'col', axis=0, tiled=True), w_in, prefer...  14.4 us
    all_to_all x1, blocking collectives, local(): lax.all_to_all(normed, 'row', split_axis=1, concat_axis=0, tiled=True)  13.7 us
    dot_general x1, matrix products, local(): jnp.dot(lax.all_gather(hidden, 'row', axis=0, tiled=True), w_out, preferr...  13.6 us
    all_to_all x1, blocking collectives, local(): lax.all_to_all(branch_out, 'row', split_axis=0, concat_axis=1, tiled=True)  12.1 us
  transfers between devices with their start and end apart: 4, of which 4 were waited for; matrix products, arithmetic and copies ran while one was open for 0% of the time, Pallas kernels for 0%

commit v1 on v0

--- a/solution.py
+++ b/solution.py
@@ -11,11 +11,13 @@
     row_var = jnp.mean(centered * centered, axis=1, keepdims=True)
     normed = (centered * lax.rsqrt(row_var + 1e-06) * ln_gain).astype(jnp.bfloat16)
     own_cols = lax.all_to_all(normed, "row", split_axis=1, concat_axis=0, tiled=True)
-    partial_pre = jnp.dot(
-        lax.all_gather(own_cols, "col", axis=0, tiled=True),
-        w_in,
-        preferred_element_type=jnp.float32,
+    step_on_columns = lambda local_x: jnp.concatenate(
+        lax.all_to_all(
+            jnp.stack([local_x for _ in range(lax.axis_size("col"))], axis=0), "col", 0, 0
+        ),
+        0,
     )
+    partial_pre = jnp.dot(step_on_columns(own_cols), w_in, preferred_element_type=jnp.float32)
     preact = lax.psum_scatter(partial_pre, "row", scatter_dimension=0, tiled=True) + b_in
     hidden = jax.nn.gelu(preact, approximate=False).astype(jnp.bfloat16)
     down_part = jnp.dot(

time: 274 us -> 267 us (0.974)
  waiting for transfers between devices: 192 us -> 168 us
  blocking collectives: 25.8 us -> 43.3 us
    all_gather x1 -> x0, waiting for transfers between devices: 23.6 us -> none  [local(): lax.all_gather(own_cols, 'col', axis=0, tiled=True)]
    all_to_all x0 -> x1, blocking collectives: none -> 17.7 us  [local(): lax.all_to_all(jnp.stack([local_x for _ in range(lax.axis_size('col'))],...]
  transfers between devices with their start and end apart: 4 -> 3, of which waited for: 4 -> 3; matrix products, arithmetic and copies ran while one was open for 0% -> 0% of each run, Pallas kernels for 0% -> 0%
where the time goes in v1:
time: 267 us
  waiting for transfers between devices  168 us (63%)
  blocking collectives  43.3 us (16%)
  matrix products  27.7 us (10%)
  other arithmetic  15 us (6%)
  between operations  13.2 us (5%)
    reduce_scatter x1, waiting for transfers between devices, local(): lax.psum_scatter(partial_pre, 'row', scatter_dimension=0, tiled=True) + b_in  99.1 us
    all_gather x1, waiting for transfers between devices, local(): lax.all_gather(hidden, 'row', axis=0, tiled=True)  46.4 us
    reduce_scatter x1, waiting for transfers between devices, local(): lax.psum_scatter(down_part.astype(jnp.bfloat16), 'col', scatter_dimension...  22 us
    all_to_all x1, blocking collectives, local(): lax.all_to_all(jnp.stack([local_x for _ in range(lax.axis_size('col'))],...  17.7 us
    dot_general x1, matrix products, local(): jnp.dot(step_on_columns(own_cols), w_in, preferred_element_type=jnp.float32)  14.2 us
    all_to_all x1, blocking collectives, local(): lax.all_to_all(normed, 'row', split_axis=1, concat_axis=0, tiled=True)  13.6 us
    dot_general x1, matrix products, local(): jnp.dot(lax.all_gather(hidden, 'row', axis=0, tiled=True), w_out, preferr...  13.6 us
    all_to_all x1, blocking collectives, local(): lax.all_to_all(branch_out, 'row', split_axis=0, concat_axis=1, tiled=True)  12.1 us
  transfers between devices with their start and end apart: 3, of which 3 were waited for; matrix products, arithmetic and copies ran while one was open for 0% of the time, Pallas kernels for 0%

profile of v1, /device:TPU:0, one launch (start us, length us, event | category | flops | bytes accessed | tf_op | source)
XLA Modules:
  0.0 267.0 jit_solution(5000225059019979598)
XLA Ops:
  6.5 0.0 reduce-scatter.3.cloned.1.call-start
  6.5 1.2 convert_reduce_fusion
  7.8 1.4 fusion.12
  9.2 1.3 fusion.14
  10.6 13.6 %all_to_all.34 = bf16[64,4,1152]{2,0,1:T(8,128)(2,1)S(1)} all-to-all(bf16[64,4,1152]{2,0,1:T(8,128)(2,1)S(1)} %bitcast.20), channel_id=1, replica_groups=mesh['grp'=4,'row'=4,'col'=2] {'row'}, dimensions={1} | all-to-all | bytes 1179648 | tf_op jit(solution)/shard_map/all_to_all | solution.py:13
  24.1 0.1 pad_maximum_fusion
  24.3 17.7 %all_to_all.35 = bf16[2,256,1152]{2,1,0:T(8,128)(2,1)S(1)} all-to-all(bf16[2,256,1152]{2,1,0:T(8,128)(2,1)S(1)} %pad_maximum_fusion), channel_id=1, replica_groups=mesh['grp'=4,'row'=4,'col'=2] {'col'}, dimensions={0} | all-to-all | bytes 2359296 | tf_op jit(solution)/shard_map/all_to_all | solution.py:15
  41.9 14.2 %fusion.16 = f32[512,6144]{1,0:T(8,128)} fusion(bf16[512,1152]{1,0:T(8,128)(2,1)S(1)} %bitcast.22, bf16[1152,6144]{1,0:T(8,128)(2,1)} %param.8), kind=kOutput, calls=%fused_computation.35 | convolution fusion | flops 7247757312 | bytes 27918336 | tf_op jit(solution)/shard_map/dot_general | solution.py:20
  56.1 0.0 copy-start.1
  56.1 0.0 reduce-scatter.3.cloned.1.call-update
  56.1 0.0 all-gather.2.cloned.1.call-start
  56.2 99.1 %reduce-scatter.3.cloned.1.call-done = f32[128,6144]{1,0:T(8,128)} async-done(((f32[512,6144]{1,0:T(8,128)}), f32[128,6144]{1,0:T(8,128)}) %reduce-scatter.3.cloned.1.call-update) | async-done | bytes 3145744 | tf_op jit(solution)/shard_map/reduce_scatter | solution.py:21
  155.3 0.0 copy-done.1
  155.3 8.8 %fusion.2 = bf16[128,6144]{1,0:T(8,128)(2,1)} fusion(f32[128,6144]{1,0:T(8,128)} %reduce-scatter.3.cloned.1.call-done, f32[6144]{0:T(1024)S(1)} %copy-done.1), kind=kLoop, calls=%fused_computation.3 | loop fusion | flops 51904512 | bytes 4743168 | tf_op jit(solution)/shard_map/convert_element_type | solution.py:22
  164.1 0.0 all-gather.2.cloned.1.call-update
  164.1 0.0 copy-start.2
  164.1 0.0 reduce-scatter.5.cloned.1.call-start
  164.2 46.4 %all-gather.2.cloned.1.call-done = bf16[512,6144]{1,0:T(8,128)(2,1)} async-done(((bf16[128,6144]{1,0:T(8,128)(2,1)}), bf16[512,6144]{1,0:T(8,128)(2,1)}) %all-gather.2.cloned.1.call-update) | async-done | bytes 6291472 | tf_op jit(solution)/shard_map/all_gather | solution.py:24
  210.6 13.6 %convolution_convert_fusion = bf16[512,1152]{1,0:T(8,128)(2,1)} fusion(bf16[512,6144]{1,0:T(8,128)(2,1)} %all-gather.2.cloned.1.call-done, bf16[6144,1152]{1,0:T(8,128)(2,1)} %param.10), kind=kOutput, calls=%fused_computation.19 | convolution fusion | flops 7248347136 | bytes 21626880 | tf_op jit(solution)/shard_map/dot_general | solution.py:23
  224.2 0.0 reduce-scatter.5.cloned.1.call-update
  224.2 0.0 copy-start
  224.2 22.0 %reduce-scatter.5.cloned.1.call-done = bf16[256,1152]{1,0:T(8,128)(2,1)} async-done(((bf16[512,1152]{1,0:T(8,128)(2,1)}), bf16[256,1152]{1,0:T(8,128)(2,1)}) %reduce-scatter.5.cloned.1.call-update) | async-done | bytes 589840 | tf_op jit(solution)/shard_map/reduce_scatter | solution.py:26
  246.2 0.0 copy-done.2
  246.2 1.2 add_convert_fusion
  247.3 12.1 %all_to_all.36 = bf16[4,64,1152]{2,1,0:T(8,128)(2,1)S(1)} all-to-all(bf16[4,64,1152]{2,1,0:T(8,128)(2,1)S(1)} %bitcast.21), channel_id=1, replica_groups=mesh['grp'=4,'row'=4,'col'=2] {'row'}, dimensions={0} | all-to-all | bytes 1179648 | tf_op jit(solution)/shard_map/all_to_all | solution.py:30
  259.4 0.1 convert_bitcast_fusion
  259.5 0.1 copy.14
  259.6 0.0 copy-done
  259.6 0.9 fusion.15
  (3 shorter events, 0.1 us)
Async XLA Ops:
  6.5 148.7 %reduce-scatter.3.cloned.1.call-start = ((), (), s32[]{:S(2)}) async-start(), calls=%async_computation.5 | async-start | bytes 15728640 | tf_op jit(solution)/shard_map/reduce_scatter | solution.py:21
  56.1 99.2 %copy-start.1 = (f32[6144]{0:T(1024)S(1)}, f32[6144]{0:T(1024)}, u32[]{:S(2)}) copy-start(f32[6144]{0:T(1024)} %param.9) | copy-start | bytes 73732
  56.1 154.5 %all-gather.2.cloned.1.call-start = ((), (), s32[]{:S(2)}) async-start(), calls=%async_computation.6 | async-start | bytes 7864320 | tf_op jit(solution)/shard_map/all_gather | solution.py:24
  164.1 82.1 %copy-start.2 = (f32[1152]{0:T(1024)S(1)}, f32[1152]{0:T(1024)}, u32[]{:S(2)}) copy-start(f32[1152]{0:T(1024)} %param.11) | copy-start | bytes 13828
  164.1 82.0 %reduce-scatter.5.cloned.1.call-start = ((), (), s32[]{:S(2)}) async-start(), calls=%async_computation.7 | async-start | bytes 1769472 | tf_op jit(solution)/shard_map/reduce_scatter | solution.py:26
  224.2 35.4 %copy-start = (bf16[64,4608]{1,0:T(8,128)(2,1)S(1)}, bf16[64,4608]{1,0:T(8,128)(2,1)}, u32[]{:S(2)}) copy-start(bf16[64,4608]{1,0:T(8,128)(2,1)} %param.6) | copy-start | bytes 1769476
Sparse Core Ops, SparseCore 0:
  56.2 98.9 reduce-scatter.2
  164.2 46.3 all-gather.1
  224.3 21.8 reduce-scatter.4
